TPU v7x, 8 devices: a whole 2x2x1 slice. The times are simulated.
8 devices in a mesh: stage: 8 (over z, y, x, core).
Axes of the slice: x: 2, y: 2, z: 1, core: 2. Of those that a mesh axis runs over, the one named last changes fastest.
Arguments:
- tokens: bfloat16 [8, 1024, 512], P('stage')
- seq_lens: int32 [8], P('stage')
- cotangent: bfloat16 [8, 1024, 512], P('stage')
- w_qkv: bfloat16 [8, 512, 1536], P('stage')
- w_out: bfloat16 [8, 512, 512], P('stage')
- w_up: bfloat16 [8, 512, 2048], P('stage')
- w_down: bfloat16 [8, 2048, 512], P('stage')
- gain_attn: bfloat16 [8, 512], P('stage')
- gain_mlp: bfloat16 [8, 512], P('stage')
Outputs:
- output 1: bfloat16 [8, 1024, 512], P('stage')
- output 2: float32 [8, 512, 1536], P('stage')
- output 3: float32 [8, 512, 512], P('stage')
- output 4: float32 [8, 512, 2048], P('stage')
- output 5: float32 [8, 2048, 512], P('stage')
- output 6: float32 [8, 512], P('stage')
- output 7: float32 [8, 512], P('stage')
All inputs are finite; a program needn't handle non-finite values.
Results may differ from a plain program's by a relative error of at most 0.02.
Values are sent between devices in bfloat16 or wider.
A program may use at most 1 GiB of HBM per device.

v0:
```python
import jax
import jax.numpy as jnp
from jax import lax
from jax.sharding import PartitionSpec as P

HEAD_DIM = 64
EPS = 1e-5
NEG_BIG = -1e9


def rms_norm(hidden, gain_vec):
    hid_f32 = hidden.astype(jnp.float32)
    inv_rms = lax.rsqrt(jnp.mean(hid_f32 * hid_f32, axis=-1, keepdims=True) + EPS)
    return (hid_f32 * inv_rms * gain_vec.astype(jnp.float32)).astype(jnp.bfloat16), inv_rms


def rms_norm_bwd(hidden, inv_rms, gain_vec, d_normed):
    scaled = hidden.astype(jnp.float32) * inv_rms
    d_gain = jnp.sum(d_normed * scaled, axis=(0, 1))
    gain_dn = d_normed * gain_vec.astype(jnp.float32)
    d_hidden = inv_rms * (gain_dn - scaled * jnp.mean(gain_dn * scaled, axis=-1, keepdims=True))
    return d_hidden, d_gain


def gelu_tanh(pre_act):
    return jax.nn.gelu(pre_act, approximate=True)


def attention_weights(q_heads, k_heads, seq_lens):
    positions = jnp.arange(q_heads.shape[1])
    scores = jnp.einsum('nqhd,nkhd->nhqk', q_heads, k_heads, preferred_element_type=jnp.float32) * (HEAD_DIM ** -0.5)
    allowed = (positions[None, None, None, :] <= positions[None, None, :, None]) & (positions[None, None, None, :] < seq_lens[:, None, None, None])
    return jax.nn.softmax(jnp.where(allowed, scores, NEG_BIG), axis=-1)


def layer_parts(hidden, seq_lens, weights):
    w_qkv, w_out, w_up, w_down, gain_attn, gain_mlp = weights
    n_seq, seq_len, model_dim = hidden.shape
    normed1, inv_rms1 = rms_norm(hidden, gain_attn)
    qkv_proj = jnp.einsum('nsd,de->nse', normed1, w_qkv, preferred_element_type=jnp.float32).astype(jnp.bfloat16)
    qkv_proj = qkv_proj.reshape(n_seq, seq_len, 3, model_dim // HEAD_DIM, HEAD_DIM)
    q_heads = qkv_proj[:, :, 0]
    k_heads = qkv_proj[:, :, 1]
    v_heads = qkv_proj[:, :, 2]
    attn_probs = attention_weights(q_heads, k_heads, seq_lens)
    probs16 = attn_probs.astype(jnp.bfloat16)
    context = jnp.einsum('nhqk,nkhd->nqhd', probs16, v_heads, preferred_element_type=jnp.float32).astype(jnp.bfloat16)
    context = context.reshape(n_seq, seq_len, model_dim)
    attn_out = jnp.einsum('nsd,de->nse', context, w_out, preferred_element_type=jnp.float32)
    mid_resid = (hidden.astype(jnp.float32) + attn_out).astype(jnp.bfloat16)
    normed2, inv_rms2 = rms_norm(mid_resid, gain_mlp)
    pre_act = jnp.einsum('nsd,df->nsf', normed2, w_up, preferred_element_type=jnp.float32)
    act16 = gelu_tanh(pre_act).astype(jnp.bfloat16)
    mlp_out = jnp.einsum('nsf,fd->nsd', act16, w_down, preferred_element_type=jnp.float32)
    layer_out = (mid_resid.astype(jnp.float32) + mlp_out).astype(jnp.bfloat16)
    saved_acts = (normed1, inv_rms1, q_heads, k_heads, v_heads, attn_probs, probs16, context, mid_resid, normed2, inv_rms2, pre_act, act16)
    return layer_out, saved_acts


def layer_backward(hidden, seq_lens, weights, d_out):
    w_qkv, w_out, w_up, w_down, gain_attn, gain_mlp = weights
    n_seq, seq_len, model_dim = hidden.shape
    saved_acts = layer_parts(hidden, seq_lens, weights)[1]
    normed1, inv_rms1, q_heads, k_heads, v_heads, attn_probs, probs16, context, mid_resid, normed2, inv_rms2, pre_act, act16 = saved_acts
    d_out16 = d_out.astype(jnp.bfloat16)
    g_down = jnp.einsum('nsf,nsd->fd', act16, d_out16, preferred_element_type=jnp.float32)
    d_act = jnp.einsum('nsd,fd->nsf', d_out16, w_down, preferred_element_type=jnp.float32)
    gelu_pullback = jax.vjp(gelu_tanh, pre_act)[1]
    d_pre16 = gelu_pullback(d_act)[0].astype(jnp.bfloat16)
    g_up = jnp.einsum('nsd,nsf->df', normed2, d_pre16, preferred_element_type=jnp.float32)
    d_normed2 = jnp.einsum('nsf,df->nsd', d_pre16, w_up, preferred_element_type=jnp.float32)
    d_mid_norm, g_gain_mlp = rms_norm_bwd(mid_resid, inv_rms2, gain_mlp, d_normed2)
    d_mid = d_out + d_mid_norm
    d_mid16 = d_mid.astype(jnp.bfloat16)
    g_out = jnp.einsum('nsd,nse->de', context, d_mid16, preferred_element_type=jnp.float32)
    d_context = jnp.einsum('nse,de->nsd', d_mid16, w_out, preferred_element_type=jnp.float32).astype(jnp.bfloat16)
    d_context = d_context.reshape(n_seq, seq_len, model_dim // HEAD_DIM, HEAD_DIM)
    d_probs = jnp.einsum('nqhd,nkhd->nhqk', d_context, v_heads, preferred_element_type=jnp.float32)
    d_value = jnp.einsum('nhqk,nqhd->nkhd', probs16, d_context, preferred_element_type=jnp.float32)
    d_scores = attn_probs * (d_probs - jnp.sum(attn_probs * d_probs, axis=-1, keepdims=True))
    d_scores16 = (d_scores * (HEAD_DIM ** -0.5)).astype(jnp.bfloat16)
    d_query = jnp.einsum('nhqk,nkhd->nqhd', d_scores16, k_heads, preferred_element_type=jnp.float32)
    d_key = jnp.einsum('nhqk,nqhd->nkhd', d_scores16, q_heads, preferred_element_type=jnp.float32)
    d_qkv = jnp.stack([d_query.astype(jnp.bfloat16), d_key.astype(jnp.bfloat16), d_value.astype(jnp.bfloat16)], axis=2).reshape(n_seq, seq_len, 3 * model_dim)
    g_qkv = jnp.einsum('nsd,nse->de', normed1, d_qkv, preferred_element_type=jnp.float32)
    d_normed1 = jnp.einsum('nse,de->nsd', d_qkv, w_qkv, preferred_element_type=jnp.float32)
    d_in_norm, g_gain_attn = rms_norm_bwd(hidden, inv_rms1, gain_attn, d_normed1)
    return d_mid + d_in_norm, (g_qkv, g_out, g_up, g_down, g_gain_attn, g_gain_mlp)


def solution(mesh):
    stages = mesh.shape['stage']
    fwd_pairs = [(source, (source - 1) % stages) for source in range(stages)]
    bwd_pairs = [(source, (source + 1) % stages) for source in range(stages)]
    home_pairs = [(source, (source + 2) % stages) for source in range(stages)]

    def pass_on(arrays, pair_list):
        return tuple(lax.ppermute(one_array, 'stage', pair_list) for one_array in arrays)

    def per_device(tokens, seq_lens, cotangent, *stage_w):
        my_stage = lax.axis_index('stage')
        own_w = tuple(weight[0] for weight in stage_w)
        n_seq, seq_len, model_dim = tokens.shape
        fwd_start = (stages - my_stage) % stages
        bwd_start = (my_stage + 1) % stages

        def fwd_compute(step_idx, loop_state):
            hidden, saved_in, held_w = loop_state
            layer_idx = step_idx - fwd_start

            def run_layer(operands):
                hid_in, saved_buf = operands
                saved_buf = lax.dynamic_update_index_in_dim(saved_buf, hid_in, layer_idx, 0)
                return layer_parts(hid_in, seq_lens, held_w)[0], saved_buf

            active = (layer_idx >= 0) & (layer_idx < stages)
            hidden, saved_in = lax.cond(active, run_layer, lambda operands: operands, (hidden, saved_in))
            return hidden, saved_in, held_w

        def fwd_body(step_idx, loop_state):
            hidden, saved_in, held_w = loop_state
            return fwd_compute(step_idx, (hidden, saved_in, pass_on(held_w, fwd_pairs)))

        saved_zero = jnp.zeros((stages, n_seq, seq_len, model_dim), jnp.bfloat16)
        loop_state = fwd_compute(0, (tokens, saved_zero, own_w))
        outputs, saved_in, _ = lax.fori_loop(1, 2 * stages - 1, fwd_body, loop_state)

        def bwd_compute(step_idx, loop_state):
            d_hidden, held_w, grad_acc = loop_state
            layer_idx = stages - 1 - (step_idx - bwd_start)

            def run_layer(operands):
                d_hid, acc_in = operands
                hid_in = lax.dynamic_index_in_dim(saved_in, layer_idx, 0, keepdims=False)
                d_prev, layer_grads = layer_backward(hid_in, seq_lens, held_w, d_hid)
                return d_prev, tuple(acc_val + grad_val for acc_val, grad_val in zip(acc_in, layer_grads))

            active = (step_idx >= bwd_start) & (step_idx < bwd_start + stages)
            d_hidden, grad_acc = lax.cond(active, run_layer, lambda operands: operands, (d_hidden, grad_acc))
            return d_hidden, held_w, grad_acc

        def bwd_body(step_idx, loop_state):
            d_hidden, held_w, grad_acc = loop_state
            return bwd_compute(step_idx, (d_hidden, pass_on(held_w, bwd_pairs), pass_on(grad_acc, bwd_pairs)))

        zero_acc = tuple(jnp.zeros(weight.shape, jnp.float32) for weight in own_w)
        loop_state = bwd_compute(0, (cotangent.astype(jnp.float32), own_w, zero_acc))
        grad_acc = lax.fori_loop(1, 2 * stages - 1, bwd_body, loop_state)[2]
        grad_home = pass_on(grad_acc, home_pairs)
        return (outputs, grad_home[0][None], grad_home[1][None], grad_home[2][None], grad_home[3][None], grad_home[4][None], grad_home[5][None])

    stage_spec = P('stage')
    return jax.shard_map(per_device, mesh=mesh, in_specs=(stage_spec,) * 9, out_specs=(stage_spec,) * 7, check_vma=False)
```

profile of v0, /device:TPU:0, one launch (start us, length us, event | category | flops | bytes accessed | tf_op | source)
XLA Modules:
  0.0 8061.6 jit_solution(15981612467227186407)
XLA Ops:
  17.9 72.1 conditional.4
  90.0 1881.0 %while.65 = (s32[]{:T(128)}, bf16[1,1024,512]{1,2,0:T(8,128)(2,1)S(1)}, bf16[8,1,1024,512]{2,3,1,0:T(8,128)(2,1)}, bf16[512,1536]{1,0:T(8,128)(2,1)}, bf16[512,5...) while((s32[]{:T(128)}, ...), condition=%wide.region_13.14_spmd, body=%wide.region_6.13_spmd.sunk | while | flops 8673825792 | bytes 136438336 | solution.py:126
  229.7 68.3 collective-permute-done
  2005.3 5715.8 %while.66 = (s32[]{:T(128)}, f32[1,1024,512]{1,2,0:T(8,128)}, bf16[512,1536]{1,0:T(8,128)(2,1)}, bf16[512,512]{1,0:T(8,128)(2,1)}, bf16[512,2048]{1,0:T(8,128)(2...) while((s32[]{:T(128)}, f32[1,1024,512]{1,2,0:T(8,128)}, ...), condition=%wide.region_37.38_spmd, body=%wide.region_25.37_spmd.sunk | while | flops 27131404288 | bytes 597161664 | solution.py:148
  2063.2 157.7 %collective-permute-done.12 = bf16[512]{0:T(512)(128)(2,1)S(1)} collective-permute-done((bf16[512]{0:T(512)(128)(2,1)S(1)}, bf16[512]{0:T(512)(128)(2,1)S(1)}, u32[]{:S(2)}, u32[]{:S(2)}) %collective-permute-start.12) | collective-permute-done | bytes 1056 | tf_op jit(solution)/shard_map/while/body/eval_jaxpr/ppermute | solution.py:98
  2323.5 181.0 %conditional.9 = ((f32[1,1024,512]{1,2,0:T(8,128)}, f32[512,1536]{1,0:T(8,128)}, f32[512,512]{1,0:T(8,128)}, f32[512,2048]{1,0:T(8,128)}, f32[2048,512]{1,0:T(8,128)}, /*index=5*/f32[512]{0:T(512)}, f32[512]{0:T(512)})) conditional(s32[]{:T(128)} %convert_element_type.785, (f32[1,1024,512]{1,2,0:T(8,128)}, f32[512,1536]{1,0:T(8,128)}, ...), branch_computations={%region_26.26_spmd, %region_27.36_spmd} | conditional | flops 27131404288 | bytes 469156608 | solution.py:139
  2520.1 116.1 %collective-permute-done.12 = bf16[512]{0:T(512)(128)(2,1)S(1)} collective-permute-done((bf16[512]{0:T(512)(128)(2,1)S(1)}, bf16[512]{0:T(512)(128)(2,1)S(1)}, u32[]{:S(2)}, u32[]{:S(2)}) %collective-permute-start.12) | collective-permute-done | bytes 1056 | tf_op jit(solution)/shard_map/while/body/eval_jaxpr/ppermute | solution.py:98
  2738.8 181.0 %conditional.9 = ((f32[1,1024,512]{1,2,0:T(8,128)}, f32[512,1536]{1,0:T(8,128)}, f32[512,512]{1,0:T(8,128)}, f32[512,2048]{1,0:T(8,128)}, f32[2048,512]{1,0:T(8,128)}, /*index=5*/f32[512]{0:T(512)}, f32[512]{0:T(512)})) conditional(s32[]{:T(128)} %convert_element_type.785, (f32[1,1024,512]{1,2,0:T(8,128)}, f32[512,1536]{1,0:T(8,128)}, ...), branch_computations={%region_26.26_spmd, %region_27.36_spmd} | conditional | flops 27131404288 | bytes 469156608 | solution.py:139
  2935.3 116.1 %collective-permute-done.12 = bf16[512]{0:T(512)(128)(2,1)S(1)} collective-permute-done((bf16[512]{0:T(512)(128)(2,1)S(1)}, bf16[512]{0:T(512)(128)(2,1)S(1)}, u32[]{:S(2)}, u32[]{:S(2)}) %collective-permute-start.12) | collective-permute-done | bytes 1056 | tf_op jit(solution)/shard_map/while/body/eval_jaxpr/ppermute | solution.py:98
  3154.0 181.0 %conditional.9 = ((f32[1,1024,512]{1,2,0:T(8,128)}, f32[512,1536]{1,0:T(8,128)}, f32[512,512]{1,0:T(8,128)}, f32[512,2048]{1,0:T(8,128)}, f32[2048,512]{1,0:T(8,128)}, /*index=5*/f32[512]{0:T(512)}, f32[512]{0:T(512)})) conditional(s32[]{:T(128)} %convert_element_type.785, (f32[1,1024,512]{1,2,0:T(8,128)}, f32[512,1536]{1,0:T(8,128)}, ...), branch_computations={%region_26.26_spmd, %region_27.36_spmd} | conditional | flops 27131404288 | bytes 469156608 | solution.py:139
  3350.5 116.1 %collective-permute-done.12 = bf16[512]{0:T(512)(128)(2,1)S(1)} collective-permute-done((bf16[512]{0:T(512)(128)(2,1)S(1)}, bf16[512]{0:T(512)(128)(2,1)S(1)}, u32[]{:S(2)}, u32[]{:S(2)}) %collective-permute-start.12) | collective-permute-done | bytes 1056 | tf_op jit(solution)/shard_map/while/body/eval_jaxpr/ppermute | solution.py:98
  3569.2 181.0 %conditional.9 = ((f32[1,1024,512]{1,2,0:T(8,128)}, f32[512,1536]{1,0:T(8,128)}, f32[512,512]{1,0:T(8,128)}, f32[512,2048]{1,0:T(8,128)}, f32[2048,512]{1,0:T(8,128)}, /*index=5*/f32[512]{0:T(512)}, f32[512]{0:T(512)})) conditional(s32[]{:T(128)} %convert_element_type.785, (f32[1,1024,512]{1,2,0:T(8,128)}, f32[512,1536]{1,0:T(8,128)}, ...), branch_computations={%region_26.26_spmd, %region_27.36_spmd} | conditional | flops 27131404288 | bytes 469156608 | solution.py:139
  3765.7 116.1 %collective-permute-done.12 = bf16[512]{0:T(512)(128)(2,1)S(1)} collective-permute-done((bf16[512]{0:T(512)(128)(2,1)S(1)}, bf16[512]{0:T(512)(128)(2,1)S(1)}, u32[]{:S(2)}, u32[]{:S(2)}) %collective-permute-start.12) | collective-permute-done | bytes 1056 | tf_op jit(solution)/shard_map/while/body/eval_jaxpr/ppermute | solution.py:98
  3984.4 181.0 %conditional.9 = ((f32[1,1024,512]{1,2,0:T(8,128)}, f32[512,1536]{1,0:T(8,128)}, f32[512,512]{1,0:T(8,128)}, f32[512,2048]{1,0:T(8,128)}, f32[2048,512]{1,0:T(8,128)}, /*index=5*/f32[512]{0:T(512)}, f32[512]{0:T(512)})) conditional(s32[]{:T(128)} %convert_element_type.785, (f32[1,1024,512]{1,2,0:T(8,128)}, f32[512,1536]{1,0:T(8,128)}, ...), branch_computations={%region_26.26_spmd, %region_27.36_spmd} | conditional | flops 27131404288 | bytes 469156608 | solution.py:139
  4180.9 116.1 %collective-permute-done.12 = bf16[512]{0:T(512)(128)(2,1)S(1)} collective-permute-done((bf16[512]{0:T(512)(128)(2,1)S(1)}, bf16[512]{0:T(512)(128)(2,1)S(1)}, u32[]{:S(2)}, u32[]{:S(2)}) %collective-permute-start.12) | collective-permute-done | bytes 1056 | tf_op jit(solution)/shard_map/while/body/eval_jaxpr/ppermute | solution.py:98
  4399.6 181.0 %conditional.9 = ((f32[1,1024,512]{1,2,0:T(8,128)}, f32[512,1536]{1,0:T(8,128)}, f32[512,512]{1,0:T(8,128)}, f32[512,2048]{1,0:T(8,128)}, f32[2048,512]{1,0:T(8,128)}, /*index=5*/f32[512]{0:T(512)}, f32[512]{0:T(512)})) conditional(s32[]{:T(128)} %convert_element_type.785, (f32[1,1024,512]{1,2,0:T(8,128)}, f32[512,1536]{1,0:T(8,128)}, ...), branch_computations={%region_26.26_spmd, %region_27.36_spmd} | conditional | flops 27131404288 | bytes 469156608 | solution.py:139
  4596.1 116.1 %collective-permute-done.12 = bf16[512]{0:T(512)(128)(2,1)S(1)} collective-permute-done((bf16[512]{0:T(512)(128)(2,1)S(1)}, bf16[512]{0:T(512)(128)(2,1)S(1)}, u32[]{:S(2)}, u32[]{:S(2)}) %collective-permute-start.12) | collective-permute-done | bytes 1056 | tf_op jit(solution)/shard_map/while/body/eval_jaxpr/ppermute | solution.py:98
  4814.8 181.0 %conditional.9 = ((f32[1,1024,512]{1,2,0:T(8,128)}, f32[512,1536]{1,0:T(8,128)}, f32[512,512]{1,0:T(8,128)}, f32[512,2048]{1,0:T(8,128)}, f32[2048,512]{1,0:T(8,128)}, /*index=5*/f32[512]{0:T(512)}, f32[512]{0:T(512)})) conditional(s32[]{:T(128)} %convert_element_type.785, (f32[1,1024,512]{1,2,0:T(8,128)}, f32[512,1536]{1,0:T(8,128)}, ...), branch_computations={%region_26.26_spmd, %region_27.36_spmd} | conditional | flops 27131404288 | bytes 469156608 | solution.py:139
  5011.3 116.1 %collective-permute-done.12 = bf16[512]{0:T(512)(128)(2,1)S(1)} collective-permute-done((bf16[512]{0:T(512)(128)(2,1)S(1)}, bf16[512]{0:T(512)(128)(2,1)S(1)}, u32[]{:S(2)}, u32[]{:S(2)}) %collective-permute-start.12) | collective-permute-done | bytes 1056 | tf_op jit(solution)/shard_map/while/body/eval_jaxpr/ppermute | solution.py:98
  5230.0 181.0 %conditional.9 = ((f32[1,1024,512]{1,2,0:T(8,128)}, f32[512,1536]{1,0:T(8,128)}, f32[512,512]{1,0:T(8,128)}, f32[512,2048]{1,0:T(8,128)}, f32[2048,512]{1,0:T(8,128)}, /*index=5*/f32[512]{0:T(512)}, f32[512]{0:T(512)})) conditional(s32[]{:T(128)} %convert_element_type.785, (f32[1,1024,512]{1,2,0:T(8,128)}, f32[512,1536]{1,0:T(8,128)}, ...), branch_computations={%region_26.26_spmd, %region_27.36_spmd} | conditional | flops 27131404288 | bytes 469156608 | solution.py:139
  5426.5 116.1 %collective-permute-done.12 = bf16[512]{0:T(512)(128)(2,1)S(1)} collective-permute-done((bf16[512]{0:T(512)(128)(2,1)S(1)}, bf16[512]{0:T(512)(128)(2,1)S(1)}, u32[]{:S(2)}, u32[]{:S(2)}) %collective-permute-start.12) | collective-permute-done | bytes 1056 | tf_op jit(solution)/shard_map/while/body/eval_jaxpr/ppermute | solution.py:98
  5660.6 176.9 %collective-permute-start.8 = (f32[512,2048]{1,0:T(8,128)}, f32[512,2048]{1,0:T(8,128)}, u32[]{:S(2)}, u32[]{:S(2)}) collective-permute-start(f32[512,2048]{1,0:T(8,128)} %get-tuple-element.1245), channel_id=1, source_target_pairs={{0,1},{1,2},{2,3},{3,4},{4,5},{5,6},{6,7},{7,0}} | collective-permute-start | bytes 12582920 | tf_op jit(solution)/shard_map/while/body/eval_jaxpr/ppermute | solution.py:98
  5839.4 69.4 collective-permute-done.12
  6068.4 181.2 %collective-permute-start.9 = (f32[2048,512]{1,0:T(8,128)}, f32[2048,512]{1,0:T(8,128)}, u32[]{:S(2)}, u32[]{:S(2)}) collective-permute-start(f32[2048,512]{1,0:T(8,128)} %get-tuple-element.1246), channel_id=1, source_target_pairs={{0,1},{1,2},{2,3},{3,4},{4,5},{5,6},{6,7},{7,0}} | collective-permute-start | bytes 12582920 | tf_op jit(solution)/shard_map/while/body/eval_jaxpr/ppermute | solution.py:98
  6275.9 86.5 %collective-permute-start.16 = (bf16[512]{0:T(512)(128)(2,1)S(1)}, bf16[512]{0:T(512)(128)(2,1)S(1)}, u32[]{:S(2)}, u32[]{:S(2)}) collective-permute-start(bf16[512]{0:T(512)(128)(2,1)S(1)} %get-tuple-element.1242), channel_id=1, source_target_pairs={{0,1},{1,2},{2,3},{3,4},{4,5},{5,6},{6,7},{7,0}} | collective-permute-start | bytes 3080 | tf_op jit(solution)/shard_map/while/body/eval_jaxpr/ppermute | solution.py:98
  6482.5 184.4 %collective-permute-start.13 = (bf16[512,1536]{1,0:T(8,128)(2,1)}, bf16[512,1536]{1,0:T(8,128)(2,1)S(1)}, u32[]{:S(2)}, u32[]{:S(2)}) collective-permute-start(bf16[512,1536]{1,0:T(8,128)(2,1)} %get-tuple-element.1237), channel_id=1, source_target_pairs={{0,1},{1,2},{2,3},{3,4},{4,5},{5,6},{6,7},{7,0}} | collective-permute-start | bytes 4718600 | tf_op jit(solution)/shard_map/while/body/eval_jaxpr/ppermute | solution.py:98
  6901.1 181.4 %collective-permute-start.14 = (bf16[512,512]{1,0:T(8,128)(2,1)}, bf16[512,512]{1,0:T(8,128)(2,1)S(1)}, u32[]{:S(2)}, u32[]{:S(2)}) collective-permute-start(bf16[512,512]{1,0:T(8,128)(2,1)} %get-tuple-element.1238), channel_id=1, source_target_pairs={{0,1},{1,2},{2,3},{3,4},{4,5},{5,6},{6,7},{7,0}} | collective-permute-start | bytes 1572872 | tf_op jit(solution)/shard_map/while/body/eval_jaxpr/ppermute | solution.py:98
  7108.7 85.2 %collective-permute-done.10 = f32[512]{0:T(512)S(1)} collective-permute-done((f32[512]{0:T(512)}, f32[512]{0:T(512)S(1)}, u32[]{:S(2)}, u32[]{:S(2)}) %collective-permute-start.10) | collective-permute-done | bytes 2080 | tf_op jit(solution)/shard_map/while/body/eval_jaxpr/ppermute | solution.py:98
  7316.8 176.9 %collective-permute-start.12 = (bf16[512]{0:T(512)(128)(2,1)S(1)}, bf16[512]{0:T(512)(128)(2,1)S(1)}, u32[]{:S(2)}, u32[]{:S(2)}) collective-permute-start(bf16[512]{0:T(512)(128)(2,1)S(1)} %get-tuple-element.1241), channel_id=1, source_target_pairs={{0,1},{1,2},{2,3},{3,4},{4,5},{5,6},{6,7},{7,0}} | collective-permute-start | bytes 3080 | tf_op jit(solution)/shard_map/while/body/eval_jaxpr/ppermute | solution.py:98
  7508.8 100.4 %collective-permute-done.10 = f32[512]{0:T(512)S(1)} collective-permute-done((f32[512]{0:T(512)}, f32[512]{0:T(512)S(1)}, u32[]{:S(2)}, u32[]{:S(2)}) %collective-permute-start.10) | collective-permute-done | bytes 2080 | tf_op jit(solution)/shard_map/while/body/eval_jaxpr/ppermute | solution.py:98
  7723.5 183.7 %collective-permute-start.18 = (f32[512,1536]{1,0:T(8,128)}, f32[512,1536]{1,0:T(8,128)}, u32[]{:S(2)}, u32[]{:S(2)}) collective-permute-start(f32[512,1536]{1,0:T(8,128)} %get-tuple-element.819), channel_id=1, source_target_pairs={{0,2},{1,3},{2,4},{3,5},{4,6},{5,7},{6,0},{7,1}} | collective-permute-start | bytes 9437192 | tf_op jit(solution)/shard_map/ppermute | solution.py:98
  7907.3 134.3 %collective-permute-done.22 = f32[512]{0:T(512)S(1)} collective-permute-done((f32[512]{0:T(512)}, f32[512]{0:T(512)S(1)}, u32[]{:S(2)}, u32[]{:S(2)}) %collective-permute-start.22) | collective-permute-done | bytes 2080 | tf_op jit(solution)/shard_map/ppermute | solution.py:98
  (1761 shorter events, 5725.1 us)
Async XLA Ops:
  2005.3 317.2 %collective-permute-start.8 = (f32[512,2048]{1,0:T(8,128)}, f32[512,2048]{1,0:T(8,128)}, u32[]{:S(2)}, u32[]{:S(2)}) collective-permute-start(f32[512,2048]{1,0:T(8,128)} %get-tuple-element.1245), channel_id=1, source_target_pairs={{0,1},{1,2},{2,3},{3,4},{4,5},{5,6},{6,7},{7,0}} | collective-permute-start | bytes 12582920 | tf_op jit(solution)/shard_map/while/body/eval_jaxpr/ppermute | solution.py:98
  2063.1 259.5 %collective-permute-start.9 = (f32[2048,512]{1,0:T(8,128)}, f32[2048,512]{1,0:T(8,128)}, u32[]{:S(2)}, u32[]{:S(2)}) collective-permute-start(f32[2048,512]{1,0:T(8,128)} %get-tuple-element.1246), channel_id=1, source_target_pairs={{0,1},{1,2},{2,3},{3,4},{4,5},{5,6},{6,7},{7,0}} | collective-permute-start | bytes 12582920 | tf_op jit(solution)/shard_map/while/body/eval_jaxpr/ppermute | solution.py:98
  2519.9 217.9 %collective-permute-start.8 = (f32[512,2048]{1,0:T(8,128)}, f32[512,2048]{1,0:T(8,128)}, u32[]{:S(2)}, u32[]{:S(2)}) collective-permute-start(f32[512,2048]{1,0:T(8,128)} %get-tuple-element.1245), channel_id=1, source_target_pairs={{0,1},{1,2},{2,3},{3,4},{4,5},{5,6},{6,7},{7,0}} | collective-permute-start | bytes 12582920 | tf_op jit(solution)/shard_map/while/body/eval_jaxpr/ppermute | solution.py:98
  2519.9 217.9 %collective-permute-start.9 = (f32[2048,512]{1,0:T(8,128)}, f32[2048,512]{1,0:T(8,128)}, u32[]{:S(2)}, u32[]{:S(2)}) collective-permute-start(f32[2048,512]{1,0:T(8,128)} %get-tuple-element.1246), channel_id=1, source_target_pairs={{0,1},{1,2},{2,3},{3,4},{4,5},{5,6},{6,7},{7,0}} | collective-permute-start | bytes 12582920 | tf_op jit(solution)/shard_map/while/body/eval_jaxpr/ppermute | solution.py:98
  2935.1 217.9 %collective-permute-start.8 = (f32[512,2048]{1,0:T(8,128)}, f32[512,2048]{1,0:T(8,128)}, u32[]{:S(2)}, u32[]{:S(2)}) collective-permute-start(f32[512,2048]{1,0:T(8,128)} %get-tuple-element.1245), channel_id=1, source_target_pairs={{0,1},{1,2},{2,3},{3,4},{4,5},{5,6},{6,7},{7,0}} | collective-permute-start | bytes 12582920 | tf_op jit(solution)/shard_map/while/body/eval_jaxpr/ppermute | solution.py:98
  2935.1 217.9 %collective-permute-start.9 = (f32[2048,512]{1,0:T(8,128)}, f32[2048,512]{1,0:T(8,128)}, u32[]{:S(2)}, u32[]{:S(2)}) collective-permute-start(f32[2048,512]{1,0:T(8,128)} %get-tuple-element.1246), channel_id=1, source_target_pairs={{0,1},{1,2},{2,3},{3,4},{4,5},{5,6},{6,7},{7,0}} | collective-permute-start | bytes 12582920 | tf_op jit(solution)/shard_map/while/body/eval_jaxpr/ppermute | solution.py:98
  3350.3 217.9 %collective-permute-start.8 = (f32[512,2048]{1,0:T(8,128)}, f32[512,2048]{1,0:T(8,128)}, u32[]{:S(2)}, u32[]{:S(2)}) collective-permute-start(f32[512,2048]{1,0:T(8,128)} %get-tuple-element.1245), channel_id=1, source_target_pairs={{0,1},{1,2},{2,3},{3,4},{4,5},{5,6},{6,7},{7,0}} | collective-permute-start | bytes 12582920 | tf_op jit(solution)/shard_map/while/body/eval_jaxpr/ppermute | solution.py:98
  3350.3 217.9 %collective-permute-start.9 = (f32[2048,512]{1,0:T(8,128)}, f32[2048,512]{1,0:T(8,128)}, u32[]{:S(2)}, u32[]{:S(2)}) collective-permute-start(f32[2048,512]{1,0:T(8,128)} %get-tuple-element.1246), channel_id=1, source_target_pairs={{0,1},{1,2},{2,3},{3,4},{4,5},{5,6},{6,7},{7,0}} | collective-permute-start | bytes 12582920 | tf_op jit(solution)/shard_map/while/body/eval_jaxpr/ppermute | solution.py:98
  3765.5 217.9 %collective-permute-start.8 = (f32[512,2048]{1,0:T(8,128)}, f32[512,2048]{1,0:T(8,128)}, u32[]{:S(2)}, u32[]{:S(2)}) collective-permute-start(f32[512,2048]{1,0:T(8,128)} %get-tuple-element.1245), channel_id=1, source_target_pairs={{0,1},{1,2},{2,3},{3,4},{4,5},{5,6},{6,7},{7,0}} | collective-permute-start | bytes 12582920 | tf_op jit(solution)/shard_map/while/body/eval_jaxpr/ppermute | solution.py:98
  3765.5 217.9 %collective-permute-start.9 = (f32[2048,512]{1,0:T(8,128)}, f32[2048,512]{1,0:T(8,128)}, u32[]{:S(2)}, u32[]{:S(2)}) collective-permute-start(f32[2048,512]{1,0:T(8,128)} %get-tuple-element.1246), channel_id=1, source_target_pairs={{0,1},{1,2},{2,3},{3,4},{4,5},{5,6},{6,7},{7,0}} | collective-permute-start | bytes 12582920 | tf_op jit(solution)/shard_map/while/body/eval_jaxpr/ppermute | solution.py:98
  4180.7 217.9 %collective-permute-start.8 = (f32[512,2048]{1,0:T(8,128)}, f32[512,2048]{1,0:T(8,128)}, u32[]{:S(2)}, u32[]{:S(2)}) collective-permute-start(f32[512,2048]{1,0:T(8,128)} %get-tuple-element.1245), channel_id=1, source_target_pairs={{0,1},{1,2},{2,3},{3,4},{4,5},{5,6},{6,7},{7,0}} | collective-permute-start | bytes 12582920 | tf_op jit(solution)/shard_map/while/body/eval_jaxpr/ppermute | solution.py:98
  4180.8 217.9 %collective-permute-start.9 = (f32[2048,512]{1,0:T(8,128)}, f32[2048,512]{1,0:T(8,128)}, u32[]{:S(2)}, u32[]{:S(2)}) collective-permute-start(f32[2048,512]{1,0:T(8,128)} %get-tuple-element.1246), channel_id=1, source_target_pairs={{0,1},{1,2},{2,3},{3,4},{4,5},{5,6},{6,7},{7,0}} | collective-permute-start | bytes 12582920 | tf_op jit(solution)/shard_map/while/body/eval_jaxpr/ppermute | solution.py:98
  4596.0 217.9 %collective-permute-start.9 = (f32[2048,512]{1,0:T(8,128)}, f32[2048,512]{1,0:T(8,128)}, u32[]{:S(2)}, u32[]{:S(2)}) collective-permute-start(f32[2048,512]{1,0:T(8,128)} %get-tuple-element.1246), channel_id=1, source_target_pairs={{0,1},{1,2},{2,3},{3,4},{4,5},{5,6},{6,7},{7,0}} | collective-permute-start | bytes 12582920 | tf_op jit(solution)/shard_map/while/body/eval_jaxpr/ppermute | solution.py:98
  5011.2 217.9 %collective-permute-start.9 = (f32[2048,512]{1,0:T(8,128)}, f32[2048,512]{1,0:T(8,128)}, u32[]{:S(2)}, u32[]{:S(2)}) collective-permute-start(f32[2048,512]{1,0:T(8,128)} %get-tuple-element.1246), channel_id=1, source_target_pairs={{0,1},{1,2},{2,3},{3,4},{4,5},{5,6},{6,7},{7,0}} | collective-permute-start | bytes 12582920 | tf_op jit(solution)/shard_map/while/body/eval_jaxpr/ppermute | solution.py:98
  5426.4 217.9 %collective-permute-start.9 = (f32[2048,512]{1,0:T(8,128)}, f32[2048,512]{1,0:T(8,128)}, u32[]{:S(2)}, u32[]{:S(2)}) collective-permute-start(f32[2048,512]{1,0:T(8,128)} %get-tuple-element.1246), channel_id=1, source_target_pairs={{0,1},{1,2},{2,3},{3,4},{4,5},{5,6},{6,7},{7,0}} | collective-permute-start | bytes 12582920 | tf_op jit(solution)/shard_map/while/body/eval_jaxpr/ppermute | solution.py:98
  5660.6 391.4 %collective-permute-start.8 = (f32[512,2048]{1,0:T(8,128)}, f32[512,2048]{1,0:T(8,128)}, u32[]{:S(2)}, u32[]{:S(2)}) collective-permute-start(f32[512,2048]{1,0:T(8,128)} %get-tuple-element.1245), channel_id=1, source_target_pairs={{0,1},{1,2},{2,3},{3,4},{4,5},{5,6},{6,7},{7,0}} | collective-permute-start | bytes 12582920 | tf_op jit(solution)/shard_map/while/body/eval_jaxpr/ppermute | solution.py:98
  6068.3 395.3 %collective-permute-start.8 = (f32[512,2048]{1,0:T(8,128)}, f32[512,2048]{1,0:T(8,128)}, u32[]{:S(2)}, u32[]{:S(2)}) collective-permute-start(f32[512,2048]{1,0:T(8,128)} %get-tuple-element.1245), channel_id=1, source_target_pairs={{0,1},{1,2},{2,3},{3,4},{4,5},{5,6},{6,7},{7,0}} | collective-permute-start | bytes 12582920 | tf_op jit(solution)/shard_map/while/body/eval_jaxpr/ppermute | solution.py:98
  6068.4 395.3 %collective-permute-start.9 = (f32[2048,512]{1,0:T(8,128)}, f32[2048,512]{1,0:T(8,128)}, u32[]{:S(2)}, u32[]{:S(2)}) collective-permute-start(f32[2048,512]{1,0:T(8,128)} %get-tuple-element.1246), channel_id=1, source_target_pairs={{0,1},{1,2},{2,3},{3,4},{4,5},{5,6},{6,7},{7,0}} | collective-permute-start | bytes 12582920 | tf_op jit(solution)/shard_map/while/body/eval_jaxpr/ppermute | solution.py:98
  6480.0 395.3 %collective-permute-start.8 = (f32[512,2048]{1,0:T(8,128)}, f32[512,2048]{1,0:T(8,128)}, u32[]{:S(2)}, u32[]{:S(2)}) collective-permute-start(f32[512,2048]{1,0:T(8,128)} %get-tuple-element.1245), channel_id=1, source_target_pairs={{0,1},{1,2},{2,3},{3,4},{4,5},{5,6},{6,7},{7,0}} | collective-permute-start | bytes 12582920 | tf_op jit(solution)/shard_map/while/body/eval_jaxpr/ppermute | solution.py:98
  6480.0 395.3 %collective-permute-start.9 = (f32[2048,512]{1,0:T(8,128)}, f32[2048,512]{1,0:T(8,128)}, u32[]{:S(2)}, u32[]{:S(2)}) collective-permute-start(f32[2048,512]{1,0:T(8,128)} %get-tuple-element.1246), channel_id=1, source_target_pairs={{0,1},{1,2},{2,3},{3,4},{4,5},{5,6},{6,7},{7,0}} | collective-permute-start | bytes 12582920 | tf_op jit(solution)/shard_map/while/body/eval_jaxpr/ppermute | solution.py:98
  6482.5 302.6 %collective-permute-start.13 = (bf16[512,1536]{1,0:T(8,128)(2,1)}, bf16[512,1536]{1,0:T(8,128)(2,1)S(1)}, u32[]{:S(2)}, u32[]{:S(2)}) collective-permute-start(bf16[512,1536]{1,0:T(8,128)(2,1)} %get-tuple-element.1237), channel_id=1, source_target_pairs={{0,1},{1,2},{2,3},{3,4},{4,5},{5,6},{6,7},{7,0}} | collective-permute-start | bytes 4718600 | tf_op jit(solution)/shard_map/while/body/eval_jaxpr/ppermute | solution.py:98
  6891.6 398.7 %collective-permute-start.8 = (f32[512,2048]{1,0:T(8,128)}, f32[512,2048]{1,0:T(8,128)}, u32[]{:S(2)}, u32[]{:S(2)}) collective-permute-start(f32[512,2048]{1,0:T(8,128)} %get-tuple-element.1245), channel_id=1, source_target_pairs={{0,1},{1,2},{2,3},{3,4},{4,5},{5,6},{6,7},{7,0}} | collective-permute-start | bytes 12582920 | tf_op jit(solution)/shard_map/while/body/eval_jaxpr/ppermute | solution.py:98
  6893.9 396.4 %collective-permute-start.9 = (f32[2048,512]{1,0:T(8,128)}, f32[2048,512]{1,0:T(8,128)}, u32[]{:S(2)}, u32[]{:S(2)}) collective-permute-start(f32[2048,512]{1,0:T(8,128)} %get-tuple-element.1246), channel_id=1, source_target_pairs={{0,1},{1,2},{2,3},{3,4},{4,5},{5,6},{6,7},{7,0}} | collective-permute-start | bytes 12582920 | tf_op jit(solution)/shard_map/while/body/eval_jaxpr/ppermute | solution.py:98
  6897.7 302.6 %collective-permute-start.13 = (bf16[512,1536]{1,0:T(8,128)(2,1)}, bf16[512,1536]{1,0:T(8,128)(2,1)S(1)}, u32[]{:S(2)}, u32[]{:S(2)}) collective-permute-start(bf16[512,1536]{1,0:T(8,128)(2,1)} %get-tuple-element.1237), channel_id=1, source_target_pairs={{0,1},{1,2},{2,3},{3,4},{4,5},{5,6},{6,7},{7,0}} | collective-permute-start | bytes 4718600 | tf_op jit(solution)/shard_map/while/body/eval_jaxpr/ppermute | solution.py:98
  6901.1 295.8 %collective-permute-start.14 = (bf16[512,512]{1,0:T(8,128)(2,1)}, bf16[512,512]{1,0:T(8,128)(2,1)S(1)}, u32[]{:S(2)}, u32[]{:S(2)}) collective-permute-start(bf16[512,512]{1,0:T(8,128)(2,1)} %get-tuple-element.1238), channel_id=1, source_target_pairs={{0,1},{1,2},{2,3},{3,4},{4,5},{5,6},{6,7},{7,0}} | collective-permute-start | bytes 1572872 | tf_op jit(solution)/shard_map/while/body/eval_jaxpr/ppermute | solution.py:98
  7306.6 396.3 %collective-permute-start.8 = (f32[512,2048]{1,0:T(8,128)}, f32[512,2048]{1,0:T(8,128)}, u32[]{:S(2)}, u32[]{:S(2)}) collective-permute-start(f32[512,2048]{1,0:T(8,128)} %get-tuple-element.1245), channel_id=1, source_target_pairs={{0,1},{1,2},{2,3},{3,4},{4,5},{5,6},{6,7},{7,0}} | collective-permute-start | bytes 12582920 | tf_op jit(solution)/shard_map/while/body/eval_jaxpr/ppermute | solution.py:98
  7309.1 393.8 %collective-permute-start.9 = (f32[2048,512]{1,0:T(8,128)}, f32[2048,512]{1,0:T(8,128)}, u32[]{:S(2)}, u32[]{:S(2)}) collective-permute-start(f32[2048,512]{1,0:T(8,128)} %get-tuple-element.1246), channel_id=1, source_target_pairs={{0,1},{1,2},{2,3},{3,4},{4,5},{5,6},{6,7},{7,0}} | collective-permute-start | bytes 12582920 | tf_op jit(solution)/shard_map/while/body/eval_jaxpr/ppermute | solution.py:98
  7312.9 296.3 %collective-permute-start.13 = (bf16[512,1536]{1,0:T(8,128)(2,1)}, bf16[512,1536]{1,0:T(8,128)(2,1)S(1)}, u32[]{:S(2)}, u32[]{:S(2)}) collective-permute-start(bf16[512,1536]{1,0:T(8,128)(2,1)} %get-tuple-element.1237), channel_id=1, source_target_pairs={{0,1},{1,2},{2,3},{3,4},{4,5},{5,6},{6,7},{7,0}} | collective-permute-start | bytes 4718600 | tf_op jit(solution)/shard_map/while/body/eval_jaxpr/ppermute | solution.py:98
  7316.3 292.8 %collective-permute-start.14 = (bf16[512,512]{1,0:T(8,128)(2,1)}, bf16[512,512]{1,0:T(8,128)(2,1)S(1)}, u32[]{:S(2)}, u32[]{:S(2)}) collective-permute-start(bf16[512,512]{1,0:T(8,128)(2,1)} %get-tuple-element.1238), channel_id=1, source_target_pairs={{0,1},{1,2},{2,3},{3,4},{4,5},{5,6},{6,7},{7,0}} | collective-permute-start | bytes 1572872 | tf_op jit(solution)/shard_map/while/body/eval_jaxpr/ppermute | solution.py:98
  7721.2 325.0 %collective-permute-start.20 = (f32[512,2048]{1,0:T(8,128)}, f32[512,2048]{1,0:T(8,128)}, u32[]{:S(2)}, u32[]{:S(2)}) collective-permute-start(f32[512,2048]{1,0:T(8,128)} %get-tuple-element.821), channel_id=1, source_target_pairs={{0,2},{1,3},{2,4},{3,5},{4,6},{5,7},{6,0},{7,1}} | collective-permute-start | bytes 12582920 | tf_op jit(solution)/shard_map/ppermute | solution.py:98
  7721.2 325.0 %collective-permute-start.21 = (f32[2048,512]{1,0:T(8,128)}, f32[2048,512]{1,0:T(8,128)}, u32[]{:S(2)}, u32[]{:S(2)}) collective-permute-start(f32[2048,512]{1,0:T(8,128)} %get-tuple-element.822), channel_id=1, source_target_pairs={{0,2},{1,3},{2,4},{3,5},{4,6},{5,7},{6,0},{7,1}} | collective-permute-start | bytes 12582920 | tf_op jit(solution)/shard_map/ppermute | solution.py:98
  7723.5 322.6 %collective-permute-start.18 = (f32[512,1536]{1,0:T(8,128)}, f32[512,1536]{1,0:T(8,128)}, u32[]{:S(2)}, u32[]{:S(2)}) collective-permute-start(f32[512,1536]{1,0:T(8,128)} %get-tuple-element.819), channel_id=1, source_target_pairs={{0,2},{1,3},{2,4},{3,5},{4,6},{5,7},{6,0},{7,1}} | collective-permute-start | bytes 9437192 | tf_op jit(solution)/shard_map/ppermute | solution.py:98
  (528 other events, 29199.8 us)
where the time goes:
time: 8080 us; the launch traced here: 8060 us
  waiting for transfers between devices  3790 us (47%)
  starting transfers between devices  1790 us (22%)
  matrix products  1690 us (21%)
  local copies, waits for them, and re-layouts  660 us (8%)
  other arithmetic  90.8 us (1%)
    ppermute x258, waiting for transfers between devices, pass_on(): lax.ppermute(one_array, 'stage', pair_list)  3790 us
    ppermute x258, starting transfers between devices, pass_on(): lax.ppermute(one_array, 'stage', pair_list)  1790 us
    while x504, local copies, waits for them, and re-layouts  505 us
    sub x16, matrix products, attention_weights(): return jax.nn.softmax(jnp.where(allowed, scores, NEG_BIG), axis=-1)  309 us
    dot_general x8, matrix products, layer_backward(): jnp.einsum('nhqk,nkhd->nqhd', d_scores16, k_heads, preferred_element_type...  267 us
    dot_general x8, matrix products, layer_backward(): jnp.einsum('nhqk,nqhd->nkhd', d_scores16, q_heads, preferred_element_type...  264 us
    dot_general x16, matrix products, layer_parts(): jnp.einsum('nhqk,nkhd->nqhd', probs16, v_heads, preferred_element_type=jn...  200 us
  transfers between devices with their start and end apart: 258, of which 113 were waited for; matrix products, arithmetic and copies ran while one was open for 3% of the time, Pallas kernels for 0%

commit v1 on v0

v1 whole, which is shorter than its diff:
```python
import functools
import jax
import jax.numpy as jnp
from jax import lax
from jax.experimental import pallas as pl
from jax.experimental.pallas import tpu as pltpu
from jax.sharding import PartitionSpec as P

bf16, f32 = jnp.bfloat16, jnp.float32
EPS = 1e-5
NEG = -1e30
NT = (((1,), (1,)), ((), ()))
MESH = pl.DeviceIdType.MESH
S, D, F, NH = 1024, 512, 2048, 8
C = 256
NC = S // C
NP = 4
KB = 128
ND = 8
LAST = ND - 1


def rms(h, g):
    r = lax.rsqrt(jnp.mean(h * h, axis=-1, keepdims=True) + EPS)
    return (h * r * g).astype(bf16)


def gelu(x):
    t = jnp.tanh(x * (0.7978845608028654 + 0.7978845608028654 * 0.044715 * (x * x)))
    hx = 0.5 * x
    return hx * t + hx


def fwd_kernel(tok, cot, ltile, wqkv, wo, w1, w2, g1, g2,
               y, cot_all, lens, sv_qkv, sv_h, sv_cx, sv_u, sv_lse,
               hbuf, st, cx_s, u_s, o_s, lse_s, k_s, vt_s, ct_s, bias, e_s, p_s,
               recv_sem, send_sem, tok_sem, len_ssem, len_rsem, cot_ssem, cot_rsem, y_sem, loc_sem, yl_sem):
    me = lax.axis_index('stage')

    barrier = pltpu.get_barrier_semaphore()
    for k in range(1, ND):
        pl.semaphore_signal(barrier, inc=1, device_id=(lax.rem(me + k, ND),), device_id_type=MESH)
    pl.semaphore_wait(barrier, ND - 1)

    def tok_copy(c):
        return pltpu.make_async_remote_copy(
            src_ref=tok.at[pl.ds(c * C, C)], dst_ref=hbuf.at[me * NC + c], send_sem=tok_sem.at[c],
            recv_sem=recv_sem.at[me * NC + c], device_id=(0,), device_id_type=MESH)

    def tok_local(c):
        return pltpu.make_async_copy(tok.at[pl.ds(c * C, C)], hbuf.at[c], recv_sem.at[c])

    def len_copy(k):
        return pltpu.make_async_remote_copy(
            src_ref=ltile, dst_ref=lens.at[me], send_sem=len_ssem.at[k - 1], recv_sem=len_rsem.at[me],
            device_id=(lax.rem(me + k, ND),), device_id_type=MESH)

    def len_wait(m):
        pltpu.make_async_remote_copy(
            src_ref=ltile, dst_ref=lens.at[m], send_sem=len_ssem.at[0], recv_sem=len_rsem.at[m],
            device_id=(0,), device_id_type=MESH).wait_recv()

    def cot_copy(m):
        return pltpu.make_async_remote_copy(
            src_ref=cot, dst_ref=cot_all.at[m], send_sem=cot_ssem.at[0], recv_sem=cot_rsem.at[m],
            device_id=(LAST,), device_id_type=MESH)

    def cot_local():
        return pltpu.make_async_copy(cot, cot_all.at[LAST], cot_ssem.at[0])

    def pass_copy(t, slot):
        return pltpu.make_async_remote_copy(
            src_ref=o_s.at[slot], dst_ref=hbuf.at[t], send_sem=send_sem.at[slot], recv_sem=recv_sem.at[t],
            device_id=(lax.rem(me + 1, ND),), device_id_type=MESH)

    def y_copy(m, c):
        return pltpu.make_async_remote_copy(
            src_ref=o_s.at[c % 2], dst_ref=y.at[pl.ds(c * C, C)], send_sem=send_sem.at[c % 2],
            recv_sem=y_sem.at[c], device_id=(m,), device_id_type=MESH)

    def y_local(c):
        return pltpu.make_async_copy(o_s.at[c % 2], y.at[pl.ds(c * C, C)], yl_sem.at[c % 2])

    def saves(m, c):
        t, slot = m * NC + c, c % 2
        rows = pl.ds(c * C, C)
        return [
            pltpu.make_async_copy(st.at[slot], sv_qkv.at[m, :, rows], loc_sem.at[slot, 0]),
            pltpu.make_async_copy(hbuf.at[t], sv_h.at[m, rows], loc_sem.at[slot, 1]),
            pltpu.make_async_copy(cx_s.at[slot], sv_cx.at[m, rows], loc_sem.at[slot, 2]),
            pltpu.make_async_copy(u_s.at[slot], sv_u.at[m, rows], loc_sem.at[slot, 3]),
            pltpu.make_async_copy(lse_s.at[slot], sv_lse.at[m, c], loc_sem.at[slot, 4]),
        ]

    def out_wait(m, c):
        @pl.when(me < LAST)
        def _():
            pass_copy(m * NC + c, c % 2).wait_send()

        @pl.when(me == LAST)
        def _():
            @pl.when(m < LAST)
            def _():
                y_copy(m, c).wait_send()

            @pl.when(m == LAST)
            def _():
                y_local(c).wait()

    @pl.when(me == 0)
    def _():
        for c in range(NC):
            tok_local(c).start()

    @pl.when(me > 0)
    def _():
        for c in range(NC):
            tok_copy(c).start()

    for k in range(1, ND):
        len_copy(k).start()
    lens[me] = ltile[...]

    def step(m, c):
        t, slot = m * NC + c, c % 2

        if c == 0:
            @pl.when(m != me)
            def _():
                len_wait(m)

        @pl.when(jnp.logical_and(me == 0, m == 0))
        def _():
            tok_local(c).wait()

        @pl.when(jnp.logical_or(me > 0, m > 0))
        def _():
            pass_copy(t, slot).wait_recv()

        def reuse(mm):
            for cp in saves(mm, (c - 2) % NC):
                cp.wait()
            out_wait(mm, (c - 2) % NC)

        if c < 2:
            @pl.when(m > 0)
            def _():
                reuse(m - 1)
        else:
            reuse(m)

        h = hbuf[t].astype(f32)
        a = rms(h, g1[...].astype(f32))
        nk = (c + 1) * C
        q = jnp.dot(a, wqkv[:, :D], preferred_element_type=f32)
        kk = jnp.dot(a, wqkv[:, D:2 * D], preferred_element_type=f32).astype(bf16)
        vv = jnp.dot(a, wqkv[:, 2 * D:], preferred_element_type=f32).astype(bf16)
        q = (q * 0.125).astype(bf16)
        for p in range(NP):
            lanes = slice(p * 128, (p + 1) * 128)
            st[slot, p] = q[:, lanes]
            st[slot, NP + p] = kk[:, lanes]
            st[slot, 2 * NP + p] = vv[:, lanes]
            k_s[p, c * C:nk] = kk[:, lanes]
            vt_s[p, :, c * C:nk] = vv[:, lanes].T

        row = lax.broadcasted_iota(jnp.int32, (C, C), 0)
        col = lax.broadcasted_iota(jnp.int32, (C, C), 1)
        ln = lens[m][0:1, :]
        for b in range(c + 1):
            ok = (row + b * C) < ln
            if b == c:
                ok = ok & (row <= col)
            bias[b * C:(b + 1) * C] = jnp.where(ok, 0.0, NEG)

        lane = lax.broadcasted_iota(jnp.int32, (C, 128), 1)

        def pair(p, carry):
            qp = st[slot, p]
            for hh in range(2):
                qm = jnp.where((lane >= 64) == (hh == 1), qp, jnp.zeros_like(qp))
                ms, ls = [], []
                nb = nk // KB
                for b in range(nb):
                    ks = slice(b * KB, (b + 1) * KB)
                    s = lax.dot_general(k_s[p, ks], qm, NT, preferred_element_type=f32) + bias[ks]
                    mb = jnp.max(s, axis=0, keepdims=True)
                    e = jnp.exp(s - mb)
                    ls.append(jnp.sum(e, axis=0, keepdims=True))
                    ms.append(mb)
                    e_s[hh, ks] = e
                mx = functools.reduce(jnp.maximum, ms)
                fs = [jnp.exp(mb - mx) for mb in ms]
                tot = sum(lb * fb for lb, fb in zip(ls, fs))
                inv = 1.0 / tot
                lse_s[slot, p, hh:hh + 1] = mx + jnp.log(tot)
                for b in range(nb):
                    ks = slice(b * KB, (b + 1) * KB)
                    p_s[hh, ks] = (e_s[hh, ks] * (fs[b] * inv)).astype(bf16)
                o = jnp.dot(vt_s[p, hh * 64:(hh + 1) * 64, 0:nk], p_s[hh, 0:nk], preferred_element_type=f32)
                ct_s[p, hh * 64:(hh + 1) * 64] = o.astype(bf16)
            return carry

        lax.fori_loop(0, NP, pair, 0, unroll=True)
        cx = jnp.concatenate([ct_s[p].T for p in range(NP)], axis=1)
        cx_s[slot] = cx
        u = (h + jnp.dot(cx, wo[...], preferred_element_type=f32)).astype(bf16)
        u_s[slot] = u
        for cp in saves(m, c):
            cp.start()
        u = u.astype(f32)
        a2 = rms(u, g2[...].astype(f32))
        z = gelu(jnp.dot(a2, w1[...], preferred_element_type=f32)).astype(bf16)
        o_s[slot] = (u + jnp.dot(z, w2[...], preferred_element_type=f32)).astype(bf16)

        @pl.when(me < LAST)
        def _():
            pass_copy(t, slot).start()

        @pl.when(me == LAST)
        def _():
            @pl.when(m < LAST)
            def _():
                y_copy(m, c).start()

            @pl.when(m == LAST)
            def _():
                y_local(c).start()

    def seq(m, carry):
        @pl.when(m == 2)
        def _():
            @pl.when(me < LAST)
            def _():
                cot_copy(me).start()

            @pl.when(me == LAST)
            def _():
                cot_local().start()

        for c in range(NC):
            step(m, c)
        return carry

    lax.fori_loop(0, ND, seq, 0)

    for c in (NC - 2, NC - 1):
        for cp in saves(LAST, c):
            cp.wait()
        out_wait(LAST, c)
    for k in range(1, ND):
        len_copy(k).wait_send()

    @pl.when(me > 0)
    def _():
        for c in range(NC):
            tok_copy(c).wait_send()

    @pl.when(me < LAST)
    def _():
        cot_copy(me).wait_send()
        for c in range(NC):
            y_copy(0, c).wait_recv()

    @pl.when(me == LAST)
    def _():
        cot_local().wait()
        for m in range(LAST):
            cot_copy(m).wait_recv()


def forward(tok, cot, ltile, wqkv, wo, w1, w2, g1, g2):
    V = pl.BlockSpec(memory_space=pltpu.VMEM)
    A = pl.BlockSpec(memory_space=pltpu.HBM)
    dma = pltpu.SemaphoreType.DMA
    sd = jax.ShapeDtypeStruct
    return pl.pallas_call(
        fwd_kernel,
        out_shape=(sd((S, D), bf16), sd((ND, S, D), bf16), sd((ND, 8, C), jnp.int32),
                   sd((ND, 3 * NP, S, 128), bf16), sd((ND, S, D), bf16), sd((ND, S, D), bf16), sd((ND, S, D), bf16),
                   sd((ND, NC, NP, 2, C), f32)),
        in_specs=[A] + [V] * 8,
        out_specs=(A, A, V, A, A, A, A, A),
        scratch_shapes=[
            pltpu.VMEM((ND * NC, C, D), bf16), pltpu.VMEM((2, 3 * NP, C, 128), bf16), pltpu.VMEM((2, C, D), bf16),
            pltpu.VMEM((2, C, D), bf16), pltpu.VMEM((2, C, D), bf16), pltpu.VMEM((2, NP, 2, C), f32),
            pltpu.VMEM((NP, S, 128), bf16), pltpu.VMEM((NP, 128, S), bf16), pltpu.VMEM((NP, 128, C), bf16),
            pltpu.VMEM((S, C), f32), pltpu.VMEM((2, S, C), f32), pltpu.VMEM((2, S, C), bf16),
            dma((ND * NC,)), dma((2,)), dma((NC,)), dma((ND - 1,)), dma((ND,)), dma((1,)), dma((ND,)), dma((NC,)),
            dma((2, 5)), dma((2,))],
        compiler_params=pltpu.CompilerParams(collective_id=0, has_side_effects=True, vmem_limit_bytes=48 * 1024 * 1024),
        cost_estimate=pl.CostEstimate(flops=80 * 10 ** 9, bytes_accessed=10 ** 8, transcendentals=10 ** 7),
    )(tok, cot, ltile, wqkv, wo, w1, w2, g1, g2)

TN = (((0,), (0,)), ((), ()))
K0 = 0.7978845608028654
K1 = K0 * 0.044715


def bwd_kernel(groups, cot_all, lens, sv_qkv, sv_h, sv_u, sv_lse, wqkv, wo, w1, w2, g1, g2,
               z_o, dpre_o, d16_o, a2_o, a_o, dmid_o, dqkv_o, gg1_o, gg2_o,
               dbuf, cbuf, qkv_b, h_b, u_b, lse_b, kt_s, dk_s, dv_s,
               z_s, dpre_s, d16_s, a2_s, a_s, dmid_s, dqkv_s, o_s, dc_s, bias, p_s, dp_s, p16_s, ds_s, dqt_s,
               recv_sem, send_sem, ld_sem, st_sem):
    me = lax.axis_index('stage')
    barrier = pltpu.get_barrier_semaphore()
    pl.semaphore_signal(barrier, inc=1, device_id=(lax.rem(me + 1, ND),), device_id_type=MESH)
    pl.semaphore_wait(barrier, 1)

    def loads(r, par, n):
        rows = pl.ds(0, n * C)
        return [
            pltpu.make_async_copy(sv_qkv.at[r, :, rows], qkv_b.at[par, :, rows], ld_sem.at[par, 0]),
            pltpu.make_async_copy(sv_h.at[r, rows], h_b.at[par, rows], ld_sem.at[par, 1]),
            pltpu.make_async_copy(sv_u.at[r, rows], u_b.at[par, rows], ld_sem.at[par, 2]),
            pltpu.make_async_copy(sv_lse.at[r, pl.ds(0, n)], lse_b.at[par, pl.ds(0, n)], ld_sem.at[par, 3]),
            pltpu.make_async_copy(cot_all.at[r, rows], cbuf.at[par, rows], ld_sem.at[par, 4]),
        ]

    def stores(row, slot):
        rows = pl.ds(row, C)
        pairs = [(z_s, z_o), (dpre_s, dpre_o), (d16_s, d16_o), (a2_s, a2_o), (a_s, a_o), (dmid_s, dmid_o), (dqkv_s, dqkv_o)]
        return [pltpu.make_async_copy(s.at[slot], o.at[rows], st_sem.at[slot, i]) for i, (s, o) in enumerate(pairs)]

    def send(t, slot):
        return pltpu.make_async_remote_copy(
            src_ref=o_s.at[slot], dst_ref=dbuf.at[t], send_sem=send_sem.at[slot], recv_sem=recv_sem.at[t],
            device_id=(lax.rem(me + ND - 1, ND),), device_id_type=MESH)

    gg1_o[...] = jnp.zeros_like(gg1_o)
    gg2_o[...] = jnp.zeros_like(gg2_o)
    for cp in loads(0, 0, groups[0][0]):
        cp.start()

    def step(r, par, c, n, base, t, slot):
        row0 = pl.multiple_of(base + c * C, C)

        def reuse():
            for cp in stores(0, slot):
                cp.wait()

            @pl.when(me > 0)
            def _():
                send(t, slot).wait_send()

        @pl.when(t >= 2)
        def _():
            reuse()

        @pl.when(me == LAST)
        def _():
            dbuf[t] = cbuf[par, c * C:(c + 1) * C].astype(f32)

        @pl.when(me < LAST)
        def _():
            send(t, slot).wait_recv()

        d = dbuf[t]
        d16 = d.astype(bf16)
        d16_s[slot] = d16
        u = u_b[par, c * C:(c + 1) * C].astype(f32)
        gm = g2[...].astype(f32)
        r2 = lax.rsqrt(jnp.mean(u * u, axis=-1, keepdims=True) + EPS)
        su = u * r2
        a2 = (su * gm).astype(bf16)
        a2_s[slot] = a2
        FB = 512
        for fb in range(F // FB):
            cols = slice(fb * FB, (fb + 1) * FB)
            x = jnp.dot(a2, w1[:, cols], preferred_element_type=f32)
            dz = lax.dot_general(d16, w2[cols], NT, preferred_element_type=f32)
            x2 = x * x
            th = jnp.tanh(x * (K0 + K1 * x2))
            hx = 0.5 * x
            z_s[slot, :, cols] = (hx * th + hx).astype(bf16)
            gp = (0.5 + 0.5 * th) + hx * (1.0 - th * th) * (K0 + 3.0 * K1 * x2)
            dpre_s[slot, :, cols] = (dz * gp).astype(bf16)
        da2 = lax.dot_general(dpre_s[slot], w1[...], NT, preferred_element_type=f32)
        gg2_o[...] += jnp.sum((da2 * su).reshape(C // 8, 8, D), axis=0)
        gd = da2 * gm
        dmid = d + r2 * (gd - su * jnp.mean(gd * su, axis=-1, keepdims=True))
        dmid16 = dmid.astype(bf16)
        dmid_s[slot] = dmid16
        o_s[slot] = dmid
        dc_s[...] = lax.dot_general(dmid16, wo[...], NT, preferred_element_type=f32).astype(bf16)

        nk = (c + 1) * C
        row = lax.broadcasted_iota(jnp.int32, (C, C), 0)
        col = lax.broadcasted_iota(jnp.int32, (C, C), 1)
        ln = lens[r][0:1, :]
        for b in range(c + 1):
            ok = (row + b * C) < ln
            if b == c:
                ok = ok & (row <= col)
            bias[b * C:(b + 1) * C] = jnp.where(ok, 0.0, NEG)
        lane = lax.broadcasted_iota(jnp.int32, (C, 128), 1)
        top = c == n - 1

        for p in range(NP):
            lanes = slice(p * 128, (p + 1) * 128)
            qp = qkv_b[par, p, c * C:(c + 1) * C]
            dcp = dc_s[:, lanes]
            for hh in range(2):
                keep = (lane >= 64) == (hh == 1)
                qm = jnp.where(keep, qp, jnp.zeros_like(qp))
                dom = jnp.where(keep, dcp, jnp.zeros_like(dcp))
                lse = lse_b[par, c, p, hh:hh + 1]
                acc = jnp.zeros((1, C), f32)
                nb = nk // KB
                for b in range(nb):
                    ks = slice(b * KB, (b + 1) * KB)
                    s = lax.dot_general(qkv_b[par, NP + p, ks], qm, NT, preferred_element_type=f32) + bias[ks]
                    pr = jnp.exp(s - lse)
                    dp = lax.dot_general(qkv_b[par, 2 * NP + p, ks], dom, NT, preferred_element_type=f32)
                    acc = acc + jnp.sum(pr * dp, axis=0, keepdims=True)
                    p16_s[hh, ks] = pr.astype(bf16)
                    p_s[hh, ks] = pr
                    dp_s[hh, ks] = dp
                for b in range(nb):
                    ks = slice(b * KB, (b + 1) * KB)
                    ds_s[hh, ks] = (p_s[hh, ks] * (dp_s[hh, ks] - acc)).astype(bf16)
                dvp = jnp.dot(p16_s[hh, 0:nk], dom, preferred_element_type=f32)
                dkp = jnp.dot(ds_s[hh, 0:nk], qm, preferred_element_type=f32)
                if top and hh == 0:
                    dv_s[p, 0:nk] = dvp
                    dk_s[p, 0:nk] = dkp
                else:
                    dv_s[p, 0:nk] += dvp
                    dk_s[p, 0:nk] += dkp
                dqt = jnp.dot(kt_s[p, hh * 64:(hh + 1) * 64, 0:nk], ds_s[hh, 0:nk], preferred_element_type=f32)
                dqt_s[p, hh * 64:(hh + 1) * 64] = dqt * 0.125
        for p in range(NP):
            for i, val in enumerate((dqt_s[p].T, dk_s[p, c * C:(c + 1) * C], dv_s[p, c * C:(c + 1) * C])):
                dqkv_s[slot, :, i * D + p * 128:i * D + (p + 1) * 128] = val.astype(bf16)
        da = lax.dot_general(dqkv_s[slot], wqkv[...], NT, preferred_element_type=f32)
        h = h_b[par, c * C:(c + 1) * C].astype(f32)
        gm = g1[...].astype(f32)
        r1 = lax.rsqrt(jnp.mean(h * h, axis=-1, keepdims=True) + EPS)
        sh = h * r1
        a_s[slot] = (sh * gm).astype(bf16)
        gg1_o[...] += jnp.sum((da * sh).reshape(C // 8, 8, D), axis=0)
        gd = da * gm
        o_s[slot] += r1 * (gd - sh * jnp.mean(gd * sh, axis=-1, keepdims=True))
        for cp in stores(row0, slot):
            cp.start()

        @pl.when(me > 0)
        def _():
            send(t, slot).start()

    r0 = t0 = 0
    for gi, (n, count) in enumerate(groups):
        nxt = groups[gi + 1][0] if gi + 1 < len(groups) else 0
        def one(i, carry, n=n, count=count, nxt=nxt, r0=r0, t0=t0):
            r = r0 + i
            par = lax.rem(r, 2)
            for cp in loads(r, par, n):
                cp.wait()

            if count > 1:
                @pl.when(i + 1 < count)
                def _():
                    for cp in loads(r + 1, 1 - par, n):
                        cp.start()
            if nxt:
                @pl.when(i + 1 == count)
                def _():
                    for cp in loads(r + 1, 1 - par, nxt):
                        cp.start()
            for p in range(NP):
                kt_s[p, :, 0:n * C] = qkv_b[par, NP + p, 0:n * C].T
            for j in range(n):
                t = t0 + i * n + j
                step(r, par, n - 1 - j, n, (t0 + i * n) * C, t, lax.rem(t, 2))
            return carry

        lax.fori_loop(0, count, one, 0)
        r0 += count
        t0 += n * count
    for t in (t0 - 2, t0 - 1):
        for cp in stores(0, t % 2):
            cp.wait()

        @pl.when(me > 0)
        def _():
            send(t, t % 2).wait_send()


def backward(groups, cid, cot_all, lens, sv_qkv, sv_h, sv_u, sv_lse, wqkv, wo, w1, w2, g1, g2):
    V = pl.BlockSpec(memory_space=pltpu.VMEM)
    A = pl.BlockSpec(memory_space=pltpu.HBM)
    dma = pltpu.SemaphoreType.DMA
    sd = jax.ShapeDtypeStruct
    T = sum(n * k for n, k in groups)
    R = T * C
    VM = pltpu.VMEM
    return pl.pallas_call(
        functools.partial(bwd_kernel, groups),
        out_shape=(sd((R, F), bf16), sd((R, F), bf16), sd((R, D), bf16), sd((R, D), bf16), sd((R, D), bf16), sd((R, D), bf16),
                   sd((R, 3 * D), bf16), sd((8, D), f32), sd((8, D), f32)),
        in_specs=[A, V] + [A] * 4 + [V] * 6,
        out_specs=(A,) * 7 + (V, V),
        scratch_shapes=[
            VM((T, C, D), f32), VM((2, S, D), bf16), VM((2, 3 * NP, S, 128), bf16), VM((2, S, D), bf16), VM((2, S, D), bf16),
            VM((2, NC, NP, 2, C), f32), VM((NP, 128, S), bf16), VM((NP, S, 128), f32), VM((NP, S, 128), f32),
            VM((2, C, F), bf16), VM((2, C, F), bf16), VM((2, C, D), bf16), VM((2, C, D), bf16), VM((2, C, D), bf16),
            VM((2, C, D), bf16), VM((2, C, 3 * D), bf16), VM((2, C, D), f32), VM((C, D), bf16), VM((S, C), f32),
            VM((2, S, C), f32), VM((2, S, C), f32), VM((2, S, C), bf16), VM((2, S, C), bf16), VM((NP, 128, C), f32),
            dma((T,)), dma((2,)), dma((2, 5)), dma((2, 7))],
        compiler_params=pltpu.CompilerParams(collective_id=cid, has_side_effects=True, vmem_limit_bytes=61 * 1024 * 1024),
        cost_estimate=pl.CostEstimate(flops=80 * 10 ** 9, bytes_accessed=10 ** 8, transcendentals=10 ** 7),
    )(cot_all, lens, sv_qkv, sv_h, sv_u, sv_lse, wqkv, wo, w1, w2, g1, g2)


def solution(mesh):
    def per_device(tokens, seq_lens, cot, wqkv, wo, w1, w2, g1, g2):
        lt = jnp.broadcast_to(seq_lens.reshape(1, 1), (8, C))
        wts = (wqkv[0], wo[0], w1[0], w2[0], g1, g2)
        y, cot_all, lens, sv_qkv, sv_h, sv_cx, sv_u, sv_lse = forward(tokens[0], cot[0], lt, *wts)
        z, dpre, d16, a2, a, dmid, dqkv, gg1, gg2 = backward(((NC, ND),), 1, cot_all, lens, sv_qkv, sv_h, sv_u, sv_lse, *wts)

        def wgrad(x, dy):
            return lax.dot_general(x, dy, TN, preferred_element_type=f32)[None]

        return (y[None], wgrad(a, dqkv), wgrad(sv_cx.reshape(-1, D), dmid), wgrad(a2, dpre), wgrad(z, d16),
                jnp.sum(gg1, axis=0, keepdims=True), jnp.sum(gg2, axis=0, keepdims=True))

    spec = P('stage')
    return jax.shard_map(per_device, mesh=mesh, in_specs=(spec,) * 9, out_specs=(spec,) * 7, check_vma=False)
```

time: 8080 us -> 793 us (0.10)
  waiting for transfers between devices: 3790 us -> 0 us
  starting transfers between devices: 1790 us -> 0 us
  matrix products: 1690 us -> 79.1 us
  Pallas kernels: 0 us -> 690 us
  local copies, waits for them, and re-layouts: 660 us -> 8.56 us
  other arithmetic: 90.8 us -> 1.19 us
    ppermute x258 -> x0, waiting for transfers between devices: 3790 us -> none  [pass_on(): lax.ppermute(one_array, 'stage', pair_list)]
    ppermute x258 -> x0, starting transfers between devices: 1790 us -> none  [pass_on(): lax.ppermute(one_array, 'stage', pair_list)]
    dot_general x152 -> x4, matrix products: 1380 us -> 79.1 us  [wgrad(): return lax.dot_general(x, dy, TN, preferred_element_type=f32)[None]]
    pallas_call x0 -> x2, Pallas kernels: none -> 690 us  [the longest x1 498 us: backward(): pl.pallas_call(functools.partial(bwd_kernel, groups), out_shape=(sd((R, F...]
    while x504 -> x0, local copies, waits for them, and re-layouts: 505 us -> none
    sub x16 -> x0, matrix products: 309 us -> none  [attention_weights(): return jax.nn.softmax(jnp.where(allowed, scores, NEG_BIG), axis=-1)]
  transfers between devices with their start and end apart: 258 -> 0, of which waited for: 113 -> 0; matrix products, arithmetic and copies ran while one was open for 3% -> 0% of each run, Pallas kernels for 0% -> 0%
where the time goes in v1:
time: 793 us; the launch traced here: 780 us
  Pallas kernels  690 us (87%)
  matrix products  79.1 us (10%)
  local copies, waits for them, and re-layouts  8.56 us (1%)
    pallas_call x1, Pallas kernels, backward(): pl.pallas_call(functools.partial(bwd_kernel, groups), out_shape=(sd((R, F...  498 us
    pallas_call x1, Pallas kernels, forward(): pl.pallas_call(fwd_kernel, out_shape=(sd((S, D), bf16), sd((ND, S, D), bf...  192 us
    dot_general x4, matrix products, wgrad(): return lax.dot_general(x, dy, TN, preferred_element_type=f32)[None]  79.1 us

profile of v1, /device:TPU:0, one launch (start us, length us, event | category | flops | bytes accessed | tf_op | source)
XLA Modules:
  0.0 779.9 jit_solution(8016831956579160434)
XLA Ops:
  1.3 0.0 copy-start
  1.3 1.4 copy-done
  2.7 0.0 copy-start.1
  2.7 1.2 copy-done.1
  3.9 0.0 copy-start.2
  3.9 1.2 copy-done.2
  5.2 0.0 copy-start.3
  5.2 1.0 copy-done.3
  6.2 0.0 copy-start.4
  6.2 0.7 copy-done.4
  6.9 0.0 copy-start.5
  6.9 0.7 copy-done.5
  7.6 192.0 %shard_map.144 = (bf16[1024,512]{1,0:T(8,128)(2,1)S(1)}, bf16[8,1024,512]{2,1,0:T(8,128)(2,1)}, s32[8,8,256]{2,1,0:T(8,128)S(1)}, bf16[8,12,1024,128]{3,2,1,0:T(...) custom-call(bf16[1024,512]{1,0:T(8,128)(2,1)S(1)} %bitcast.31, ...), custom_call_target="tpu_custom_call" | custom-call | flops 80000000000 | bytes 100000000 | tf_op jit(solution)/shard_map/pallas_call | solution.py:277
  199.5 0.0 copy-start.6
  199.6 0.7 copy-done.6
  200.2 0.0 copy-start.7
  200.3 0.6 copy-done.7
  200.9 497.6 %shard_map.145 = (bf16[8192,2048]{1,0:T(8,128)(2,1)}, bf16[8192,2048]{1,0:T(8,128)(2,1)}, bf16[8192,512]{1,0:T(8,128)(2,1)}, bf16[8192,512]{1,0:T(8,128)(2,1)}, ...) custom-call(bf16[8,1024,512]{2,1,0:T(8,128)(2,1)} %get-tuple-element, ...), custom_call_target="tpu_custom_call" | custom-call | flops 80000000000 | bytes 100000000 | tf_op jit(solution)/shard_map/pallas_call | solution.py:497
  698.5 0.0 copy-start.10
  698.5 11.4 %convolution_bitcast_fusion.3 = f32[1,512,512]{2,1,0:T(8,128)} fusion(bf16[8192,512]{1,0:T(8,128)(2,1)} %bitcast.41, bf16[8192,512]{1,0:T(8,128)(2,1)} %get-tuple-element.34), kind=kOutput, calls=%fused_computation.3 | convolution fusion | flops 4294967296 | bytes 17825792 | tf_op jit(solution)/shard_map/dot_general | solution.py:523
  709.9 0.0 copy-done.10
  709.9 0.0 copy-start.9
  709.9 0.0 copy-start.8
  709.9 18.0 %convolution_bitcast_fusion.2 = f32[1,512,1536]{2,1,0:T(8,128)} fusion(bf16[8192,512]{1,0:T(8,128)(2,1)S(1)} %copy-done.10, bf16[8192,1536]{1,0:T(8,128)(2,1)} %get-tuple-element.32), kind=kOutput, calls=%fused_computation.2 | convolution fusion | flops 12884901888 | bytes 36700160 | tf_op jit(solution)/shard_map/dot_general | solution.py:523
  727.9 0.0 copy-done.9
  727.9 0.6 reduce_sum.18
  728.5 0.0 copy-done.8
  728.5 0.6 reduce_sum.19
  729.1 24.8 %convolution_bitcast_fusion.1 = f32[1,512,2048]{2,1,0:T(8,128)} fusion(bf16[8192,512]{1,0:T(8,128)(2,1)} %get-tuple-element.35, bf16[8192,2048]{1,0:T(8,128)(2,1)} %get-tuple-element.36), kind=kOutput, calls=%fused_computation.1 | convolution fusion | flops 17179869184 | bytes 46137344 | tf_op jit(solution)/shard_map/dot_general | solution.py:523
  753.9 24.8 %convolution_bitcast_fusion = f32[1,2048,512]{2,1,0:T(8,128)} fusion(bf16[8192,2048]{1,0:T(8,128)(2,1)} %get-tuple-element.37, bf16[8192,512]{1,0:T(8,128)(2,1)} %get-tuple-element.38), kind=kOutput, calls=%fused_computation | convolution fusion | flops 17179869184 | bytes 46137344 | tf_op jit(solution)/shard_map/dot_general | solution.py:523
  778.7 1.0 copy.18
  (1 shorter events, 0.0 us)
Async XLA Ops:
  1.3 1.4 copy-start
  2.7 1.2 copy-start.1
  3.9 1.2 copy-start.2
  5.2 1.0 copy-start.3
  6.2 0.7 copy-start.4
  6.9 0.7 copy-start.5
  199.5 0.7 copy-start.6
  200.2 0.6 copy-start.7
  698.5 11.4 %copy-start.10 = (bf16[8192,512]{1,0:T(8,128)(2,1)S(1)}, bf16[8192,512]{1,0:T(8,128)(2,1)}, u32[]{:S(2)}) copy-start(bf16[8192,512]{1,0:T(8,128)(2,1)} %get-tuple-element.31) | copy-start | bytes 25165828
  709.9 18.0 %copy-start.9 = (f32[8,512]{1,0:T(8,128)S(1)}, f32[8,512]{1,0:T(8,128)}, u32[]{:S(2)}) copy-start(f32[8,512]{1,0:T(8,128)} %get-tuple-element.39) | copy-start | bytes 49156
  709.9 18.6 %copy-start.8 = (f32[8,512]{1,0:T(8,128)S(1)}, f32[8,512]{1,0:T(8,128)}, u32[]{:S(2)}) copy-start(f32[8,512]{1,0:T(8,128)} %get-tuple-element.40) | copy-start | bytes 49156
